TPU v7x, 32 devices: a whole 2x2x4 slice. The times are simulated.
32 devices in a mesh: span: 8 (over y, x, core), head: 4 (over z), rep: 1.
Axes of the slice: x: 2, y: 2, z: 4, core: 2. Of those that a mesh axis runs over, the one named last changes fastest.
Arguments:
- queries: bfloat16 [4096, 4096], P(('rep', 'span', 'head')), may hold values from -9 to 9
- keys: bfloat16 [4096, 512], P(('rep', 'span', 'head')), may hold values from -9 to 9
- values: bfloat16 [4096, 512], P(('rep', 'span', 'head')), may hold values from -6 to 6
- out_grad: bfloat16 [4096, 4096], P(('rep', 'span'), 'head'), may hold values from -6 to 6
- doc_lengths: int32 [4], P('rep'), may hold values from 1 to 2048, 4096 in all
Outputs:
- key_value_grads: bfloat16 [1024, 4096], P('head', ('rep', 'span'))
- log_totals: float32 [32, 4096], P('head', ('rep', 'span'))
Inputs may be any that keep to these rules, and one draw needn't show every extreme that they name: `doc_lengths`: they sum to 4096; the longest is exactly 2048.
All inputs are finite; a program needn't handle non-finite values.
Results may differ from a plain program's by a relative error of at most 0.0068.
Values may be sent and summed in bfloat16 or wider, within the bound.
A program may use at most 64 MiB of HBM per device.

v0:
```python
import math

import jax
import jax.numpy as jnp
from jax import lax
from jax.experimental import pallas as pl
from jax.experimental.pallas import tpu as pltpu
from jax.sharding import PartitionSpec as P

HEADS = 32
KV_HEADS = 4
HEAD_DIM = 128
BLOCK = 128
WINDOW = 2
HALO = 128
LOG2E = math.log2(math.e)
LN2 = math.log(2.0)
MESH = pl.DeviceIdType.MESH


def from_partner(block, axis, bit):
    count = lax.axis_size(axis)
    route = []
    for low in range(count):
        high = low | 1 << bit
        if high != low and high < count:
            route += [(low, high), (high, low)]
    return lax.ppermute(block, axis, route)


def passed_along(block, axis, distance):
    devices = range(lax.axis_size(axis))
    route = [(i - distance, i) for i in devices if i - distance in devices]
    return lax.ppermute(block, axis, route)


def group_total(partial_value, sharers, head_index):
    levels = sharers.bit_length() - 1
    for level in reversed(range(levels)):
        half_rows = partial_value.shape[0] // 2
        lower_half = head_index >> level & 1 == 0
        kept_rows = jnp.where(lower_half, partial_value[:half_rows], partial_value[half_rows:])
        given_rows = jnp.where(lower_half, partial_value[half_rows:], partial_value[:half_rows])
        partial_value = kept_rows + from_partner(given_rows, "head", level)
    return partial_value


def shards(queries, keys, values, out_grad, doc_lengths):
    head_count = lax.axis_size("head")
    head_index = lax.axis_index("head")
    span_index = lax.axis_index("span")
    tok_rows = queries.shape[0]
    heads_here = HEADS // head_count
    sharers = head_count // KV_HEADS
    span_len = tok_rows * head_count
    score_scale = 1.0 / math.sqrt(HEAD_DIM)
    query_send = queries.reshape(tok_rows, head_count, heads_here * HEAD_DIM)
    keyval = jnp.concatenate(
        [keys.reshape(tok_rows, KV_HEADS, HEAD_DIM), values.reshape(tok_rows, KV_HEADS, HEAD_DIM)],
        axis=2,
    )
    repeated = jnp.repeat(keyval, sharers, axis=1)
    query_local, pairs_local = (
        lax.all_to_all(query_send, "head", split_axis=1, concat_axis=0, tiled=True),
        lax.all_to_all(repeated, "head", split_axis=1, concat_axis=0, tiled=True),
    )
    pairs_local = pairs_local.reshape(span_len, 2 * HEAD_DIM)
    query_local = query_local.reshape(span_len, heads_here, HEAD_DIM)
    grad_local = out_grad.reshape(span_len, heads_here, HEAD_DIM)
    earlier = passed_along(pairs_local[span_len - HALO :], "span", 1)
    extended = jnp.concatenate([earlier, pairs_local], 0)
    base_row = span_index * span_len
    doc_starts = jnp.cumsum(doc_lengths) - doc_lengths
    query_pos = base_row + jnp.arange(span_len, dtype=jnp.int32)
    doc_first = jnp.max(
        jnp.where(doc_starts[None, :] <= query_pos[:, None], doc_starts[None, :], 0), axis=1
    )
    n_blocks = span_len // BLOCK
    per_group = min(n_blocks, max(1, 512 // BLOCK))
    n_groups = n_blocks // per_group
    group_rows = per_group * BLOCK
    width = WINDOW * BLOCK
    block_offsets = jnp.arange(BLOCK, dtype=jnp.int32)
    window_offsets = jnp.arange(width, dtype=jnp.int32)
    block_starts = jnp.arange(per_group, dtype=jnp.int32) * BLOCK

    def attend(gradients, group_index):
        first_row = group_index * group_rows
        query_group = lax.dynamic_slice_in_dim(query_local, first_row, group_rows, 0).reshape(
            per_group, BLOCK, heads_here, HEAD_DIM
        )
        grad_group = lax.dynamic_slice_in_dim(grad_local, first_row, group_rows, 0).reshape(
            per_group, BLOCK, heads_here, HEAD_DIM
        )
        pair_rows = lax.dynamic_slice_in_dim(extended, first_row, group_rows + HALO, 0).reshape(
            per_group + WINDOW - 1, BLOCK, 2 * HEAD_DIM
        )
        window = jnp.stack(
            [pair_rows[shift_index : shift_index + per_group] for shift_index in range(WINDOW)],
            axis=1,
        ).reshape(per_group, width, 2 * HEAD_DIM)
        key_window = window[..., :HEAD_DIM]
        value_window = window[..., HEAD_DIM:]
        query_rows = base_row + first_row + block_starts[:, None] + block_offsets[None, :]
        key_rows = base_row + first_row - HALO + block_starts[:, None] + window_offsets[None, :]
        first_doc = lax.dynamic_slice_in_dim(doc_first, first_row, group_rows, 0).reshape(
            per_group, BLOCK
        )
        allowed = (key_rows[:, None, :] >= first_doc[:, :, None]) & (
            key_rows[:, None, :] <= query_rows[:, :, None]
        )
        scores = (
            jnp.einsum(
                "gqhd,gkd->ghqk", query_group, key_window, preferred_element_type=jnp.float32
            )
            * score_scale
        )
        scores = jnp.where(allowed[:, None], scores, -1e30)
        row_max = jnp.max(scores, axis=-1, keepdims=True)
        exponent = jnp.exp(scores - row_max)
        row_total = jnp.sum(exponent, axis=-1, keepdims=True)
        weights = exponent / row_total
        log_totals = (row_max + jnp.log(row_total))[..., 0]
        weights_low = weights.astype(jnp.bfloat16)
        attention = jnp.einsum(
            "ghqk,gkd->gqhd", weights_low, value_window, preferred_element_type=jnp.float32
        ).astype(jnp.bfloat16)
        attention = lax.optimization_barrier(attention).astype(jnp.float32)
        dweights = jnp.einsum(
            "gqhd,gkd->ghqk", grad_group, value_window, preferred_element_type=jnp.float32
        )
        delta_rows = jnp.einsum("gqhd,gqhd->ghq", grad_group.astype(jnp.float32), attention)
        dscores = (weights * (dweights - delta_rows[..., None])).astype(jnp.bfloat16)
        key_part = (
            jnp.einsum("ghqk,gqhd->gkd", dscores, query_group, preferred_element_type=jnp.float32)
            * score_scale
        )
        value_part = jnp.einsum(
            "ghqk,gqhd->gkd", weights_low, grad_group, preferred_element_type=jnp.float32
        )
        pieces = jnp.concatenate([key_part, value_part], -1).reshape(
            per_group, WINDOW, BLOCK, 2 * HEAD_DIM
        )
        folded = jnp.zeros((per_group + WINDOW - 1, BLOCK, 2 * HEAD_DIM), jnp.float32)
        for shift_index in range(WINDOW):
            folded = folded.at[shift_index : shift_index + per_group].add(pieces[:, shift_index])
        folded = folded.reshape(group_rows + HALO, 2 * HEAD_DIM)
        current = lax.dynamic_slice_in_dim(gradients, first_row, group_rows + HALO, 0)
        gradients = lax.dynamic_update_slice_in_dim(gradients, current + folded, first_row, 0)
        return (gradients, jnp.transpose(log_totals, (1, 0, 2)).reshape(heads_here, group_rows))

    gradients, total_groups = lax.scan(
        attend,
        jnp.zeros((HALO + span_len, 2 * HEAD_DIM), jnp.float32),
        jnp.arange(n_groups, dtype=jnp.int32),
    )
    log_totals = jnp.transpose(total_groups, (1, 0, 2)).reshape(heads_here, span_len)
    summed = group_total(gradients.T, sharers, head_index)
    returned = passed_along(summed[:, :HALO].astype(jnp.bfloat16), "span", -1).astype(jnp.float32)
    local_grads = summed[:, HALO:].at[:, span_len - HALO :].add(returned)
    return (local_grads.astype(jnp.bfloat16), log_totals)


def attend_kernel(
    lengths, queries, keys, values, out_grad,
    grads_out, totals_out,
    query_buf, key_buf, value_buf, query_slots, key_ext, value_ext, grad_buf,
    bias, key_acc, value_acc, halo_send, halo_recv, total_rows,
    local_sems, pair_send, pair_recv, query_send, query_recv, edge_send, edge_recv,
):
    span = lax.axis_index("span")
    spans = lax.axis_size("span")
    me = lax.axis_index("head")
    peers = lax.axis_size("head")
    last = peers - 1
    rows = queries.shape[0]
    head_cols = queries.shape[1] // peers
    piece_cols = 2 * HEAD_DIM
    pieces = head_cols // piece_cols
    width = WINDOW * BLOCK
    swapped = me + 1 - 2 * lax.rem(me, 2)
    order = (me, swapped, last - swapped, last - me)
    targets = (last - swapped, swapped, last - me)

    def column(index, size):
        return pl.ds(pl.multiple_of(index * size, size), size)

    own_rows = pl.ds(pl.multiple_of(HALO + me * rows, rows), rows)
    loads = [
        pltpu.make_async_copy(keys, key_buf, local_sems.at[0]),
        pltpu.make_async_copy(values, value_buf, local_sems.at[1]),
        pltpu.make_async_copy(queries, query_buf, local_sems.at[2]),
        pltpu.make_async_copy(
            keys.at[:, column(me, HEAD_DIM)], key_ext.at[own_rows], local_sems.at[3]
        ),
        pltpu.make_async_copy(
            values.at[:, column(me, HEAD_DIM)], value_ext.at[own_rows], local_sems.at[4]
        ),
        pltpu.make_async_copy(
            queries.at[:, column(me, head_cols)], query_slots.at[me], local_sems.at[5]
        ),
        pltpu.make_async_copy(out_grad, grad_buf, local_sems.at[6]),
    ]
    for load in loads:
        load.start()

    barrier = pltpu.get_barrier_semaphore()
    for peer in order[1:]:
        pl.semaphore_signal(barrier, inc=1, device_id={"head": peer}, device_id_type=MESH)

    @pl.when(span > 0)
    def _():
        pl.semaphore_signal(barrier, inc=1, device_id={"span": span - 1}, device_id_type=MESH)

    @pl.when(span < spans - 1)
    def _():
        pl.semaphore_signal(barrier, inc=1, device_id={"span": span + 1}, device_id_type=MESH)

    neighbours = jnp.minimum(span, 1) + jnp.minimum(spans - 1 - span, 1)
    pl.semaphore_wait(barrier, peers - 1 + neighbours)

    def pair_copy(which, buf, ext, source, target):
        return pltpu.make_async_remote_copy(
            src_ref=buf.at[:, column(target, HEAD_DIM)],
            dst_ref=ext.at[pl.ds(pl.multiple_of(HALO + source * rows, rows), rows)],
            send_sem=pair_send.at[which, target],
            recv_sem=pair_recv.at[which, source],
            device_id={"head": target},
            device_id_type=MESH,
        )

    def query_copy(piece, source, target):
        return pltpu.make_async_remote_copy(
            src_ref=query_buf.at[:, column(target * pieces + piece, piece_cols)],
            dst_ref=query_slots.at[source, :, column(piece, piece_cols)],
            send_sem=query_send.at[target, piece],
            recv_sem=query_recv.at[source, piece],
            device_id={"head": target},
            device_id_type=MESH,
        )

    loads[0].wait()
    loads[1].wait()
    for peer in targets:
        pair_copy(0, key_buf, key_ext, me, peer).start()
        pair_copy(1, value_buf, value_ext, me, peer).start()
    loads[2].wait()
    for peer in targets:
        for piece in range(pieces):
            query_copy(piece, me, peer).start()


    key_acc[...] = jnp.zeros_like(key_acc)
    value_acc[...] = jnp.zeros_like(value_acc)
    for load in loads[3:]:
        load.wait()
    for peer in order[1:]:
        pair_copy(0, key_buf, key_ext, peer, me).wait_recv()
        pair_copy(1, value_buf, value_ext, peer, me).wait_recv()

    def halo_copy(which, ext):
        return pltpu.make_async_remote_copy(
            src_ref=ext.at[pl.ds(peers * rows, HALO)],
            dst_ref=ext.at[pl.ds(0, HALO)],
            send_sem=edge_send.at[which],
            recv_sem=edge_recv.at[which],
            device_id={"span": span + 1},
            device_id_type=MESH,
        )

    return_copy = pltpu.make_async_remote_copy(
        src_ref=halo_send,
        dst_ref=halo_recv,
        send_sem=edge_send.at[2],
        recv_sem=edge_recv.at[2],
        device_id={"span": span - 1},
        device_id_type=MESH,
    )

    @pl.when(span < spans - 1)
    def _():
        halo_copy(0, key_ext).start()
        halo_copy(1, value_ext).start()

    @pl.when(span > 0)
    def _():
        halo_copy(0, key_ext).wait_recv()
        halo_copy(1, value_ext).wait_recv()

    @pl.when(span == 0)
    def _():
        key_ext[pl.ds(0, HALO)] = jnp.zeros((HALO, HEAD_DIM), jnp.bfloat16)
        value_ext[pl.ds(0, HALO)] = jnp.zeros((HALO, HEAD_DIM), jnp.bfloat16)

    score_scale = 1.0 / math.sqrt(HEAD_DIM)
    contract_last = (((1,), (1,)), ((), ()))

    def stacked(block):
        return jnp.concatenate([block[:, :HEAD_DIM], block[:, HEAD_DIM:]], axis=0)

    def write(done):
        held = pl.ds(HALO + done * BLOCK, BLOCK)
        cols = pl.ds(done * BLOCK, BLOCK)
        key_part = key_acc[held] * score_scale
        grads_out[pl.ds(0, HEAD_DIM), cols] = key_part.T.astype(jnp.bfloat16)
        grads_out[pl.ds(HEAD_DIM, HEAD_DIM), cols] = value_acc[held].T.astype(jnp.bfloat16)

    for step in range(4):
        block = order[step]
        first_row = pl.multiple_of(block * BLOCK, BLOCK)
        window = pl.ds(first_row, width)
        base = (span * peers + block) * BLOCK
        query_pos = base + lax.broadcasted_iota(jnp.int32, (1, BLOCK), 1)
        first = jnp.zeros((1, BLOCK), jnp.int32)
        start = jnp.int32(0)
        for doc in range(lengths.shape[0]):
            first = jnp.maximum(first, jnp.where(query_pos >= start, start, 0))
            start = start + lengths[doc]
        key_pos = base - HALO + lax.broadcasted_iota(jnp.int32, (width, BLOCK), 0)
        allowed = (key_pos >= first) & (key_pos <= query_pos)
        bias[...] = jnp.where(allowed, 0.0, -1e30)

        def one_piece(piece, carry, block=block, first_row=first_row, window=window, step=step):
            if step > 0:
                query_copy(piece, block, me).wait_recv()
            cols = column(piece, piece_cols)
            query_pair = stacked(query_slots[block, :, cols])
            grad_pair = stacked(grad_buf[pl.ds(first_row, BLOCK), cols])
            scores = lax.dot_general(
                key_ext[window], query_pair, contract_last, preferred_element_type=jnp.float32
            )
            dweights = lax.dot_general(
                value_ext[window], grad_pair, contract_last, preferred_element_type=jnp.float32
            )
            shift = bias[...]
            scores = scores * (score_scale * LOG2E) + jnp.concatenate([shift, shift], axis=1)
            row_max = jnp.max(scores, axis=0, keepdims=True)
            exponent = jnp.exp2(scores - row_max)
            row_total = jnp.sum(exponent, axis=0, keepdims=True)
            weights = exponent * (1.0 / row_total)
            weights_low = weights.astype(jnp.bfloat16)
            delta = jnp.sum(weights * dweights, axis=0, keepdims=True)
            dscores = (weights * (dweights - delta)).astype(jnp.bfloat16)
            key_acc[window] += jnp.dot(dscores, query_pair, preferred_element_type=jnp.float32)
            value_acc[window] += jnp.dot(weights_low, grad_pair, preferred_element_type=jnp.float32)
            totals = row_max * LN2 + jnp.log(row_total)
            for half in range(2):
                total_rows[block * pieces + piece, half : half + 1] = totals[
                    :, half * BLOCK : (half + 1) * BLOCK
                ]
            return carry

        if step == 3:
            for done in range(peers - 1):

                @pl.when((done != block) & (done != block - 1))
                def _():
                    write(done)

        lax.fori_loop(0, pieces, one_piece, 0)

        @pl.when((block == 0) & (span > 0))
        def _():
            halo_send[pl.ds(0, HALO)] = key_acc[pl.ds(0, HALO)].astype(jnp.bfloat16)
            halo_send[pl.ds(HALO, HALO)] = value_acc[pl.ds(0, HALO)].astype(jnp.bfloat16)
            return_copy.start()

    for block in range(peers):
        for head in range(2 * pieces):
            totals_out[head : head + 1, block * BLOCK : (block + 1) * BLOCK] = total_rows[
                block * pieces + head // 2, head % 2 : head % 2 + 1
            ]

    for done in range(peers - 1):

        @pl.when((done == order[3]) | (done == order[3] - 1))
        def _():
            write(done)

    @pl.when(span < spans - 1)
    def _():
        return_copy.wait_recv()
        held = pl.ds(last * BLOCK + HALO, BLOCK)
        returned = halo_recv[...].astype(jnp.float32)
        key_acc[held] += returned[:HALO]
        value_acc[held] += returned[HALO:]

    write(last)

    for peer in order[1:]:
        pair_copy(0, key_buf, key_ext, me, peer).wait_send()
        pair_copy(1, value_buf, value_ext, me, peer).wait_send()
        for piece in range(pieces):
            query_copy(piece, me, peer).wait_send()

    @pl.when(span < spans - 1)
    def _():
        halo_copy(0, key_ext).wait_send()
        halo_copy(1, value_ext).wait_send()

    @pl.when(span > 0)
    def _():
        return_copy.wait_send()


def put_out(grads, totals, grads_out, totals_out, sems):
    copies = [
        pltpu.make_async_copy(grads, grads_out, sems.at[0]),
        pltpu.make_async_copy(totals, totals_out, sems.at[1]),
    ]
    for copy in copies:
        copy.start()
    for copy in copies:
        copy.wait()


def fused_shards(queries, keys, values, out_grad, doc_lengths):
    head_count = lax.axis_size("head")
    rows = queries.shape[0]
    span_len = rows * head_count
    head_cols = queries.shape[1] // head_count
    heads_here = HEADS // head_count
    pieces = heads_here // 2
    any_space = pl.BlockSpec(memory_space=pl.ANY)
    vmem = pl.BlockSpec(memory_space=pltpu.VMEM)
    dma = pltpu.SemaphoreType.DMA
    held = pl.pallas_call(
        attend_kernel,
        out_shape=(
            pltpu.VMEM((2 * HEAD_DIM, span_len), jnp.bfloat16),
            pltpu.VMEM((heads_here, span_len), jnp.float32),
        ),
        in_specs=[pl.BlockSpec(memory_space=pltpu.SMEM)] + [any_space] * 4,
        out_specs=(vmem, vmem),
        scratch_shapes=[
            pltpu.VMEM(queries.shape, jnp.bfloat16),
            pltpu.VMEM(keys.shape, jnp.bfloat16),
            pltpu.VMEM(values.shape, jnp.bfloat16),
            pltpu.VMEM((head_count, rows, head_cols), jnp.bfloat16),
            pltpu.VMEM((HALO + span_len, HEAD_DIM), jnp.bfloat16),
            pltpu.VMEM((HALO + span_len, HEAD_DIM), jnp.bfloat16),
            pltpu.VMEM(out_grad.shape, jnp.bfloat16),
            pltpu.VMEM((WINDOW * BLOCK, BLOCK), jnp.float32),
            pltpu.VMEM((HALO + span_len, HEAD_DIM), jnp.float32),
            pltpu.VMEM((HALO + span_len, HEAD_DIM), jnp.float32),
            pltpu.VMEM((2 * HALO, HEAD_DIM), jnp.bfloat16),
            pltpu.VMEM((2 * HALO, HEAD_DIM), jnp.bfloat16),
            pltpu.VMEM((head_count * pieces, 8, BLOCK), jnp.float32),
            dma((7,)),
            dma((2, head_count)),
            dma((2, head_count)),
            dma((head_count, pieces)),
            dma((head_count, pieces)),
            dma((3,)),
            dma((3,)),
        ],
        compiler_params=pltpu.CompilerParams(collective_id=0, has_side_effects=True),
        name="attend",
    )(doc_lengths, queries, keys, values, out_grad)
    return pl.pallas_call(
        put_out,
        out_shape=tuple(jax.ShapeDtypeStruct(one.shape, one.dtype) for one in held),
        in_specs=[vmem, vmem],
        out_specs=(any_space, any_space),
        scratch_shapes=[dma((2,))],
        name="put_out",
    )(*[pltpu.with_memory_space_constraint(one, pltpu.VMEM) for one in held])


def pick_shards(queries, keys, values, out_grad, doc_lengths):
    head_count = lax.axis_size("head")
    if head_count == KV_HEADS == 4 and queries.shape[0] == BLOCK == HALO:
        return fused_shards(queries, keys, values, out_grad, doc_lengths)
    return shards(queries, keys, values, out_grad, doc_lengths)


def solution(mesh):
    return jax.shard_map(
        pick_shards,
        mesh=mesh,
        in_specs=(
            P(("rep", "span", "head"), None),
            P(("rep", "span", "head"), None),
            P(("rep", "span", "head"), None),
            P(("rep", "span"), "head"),
            P("rep"),
        ),
        out_specs=(P("head", ("rep", "span")), P("head", ("rep", "span"))),
        check_vma=False,
    )
```

profile of v0, /device:TPU:25, one launch (start us, length us, event | category | flops | bytes accessed | tf_op | source)
XLA Modules:
  0.0 36.3 jit_solution(1497536518934566843)
XLA Ops:
  0.6 35.0 %attend.1 = (bf16[256,512]{1,0:T(8,128)(2,1)S(1)}, f32[8,512]{1,0:T(8,128)S(1)}) custom-call(s32[4]{0:T(128)} %lengths.1, bf16[128,4096]{1,0:T(8,128)(2,1)} %queries.1, bf16[128,512]{1,0:T(8,128)(2,1)} %keys.1, bf16[128,512]{1,0:T(8,128)(2,1)} %values.1, bf16[512,1024]{1,0:T(8,128)(2,1)} %out_grad.1), custom_call_target="tpu_custom_call" | custom-call | tf_op jit(solution)/shard_map/attend/pallas_call | solution.py:427
  35.6 0.7 %put_out.1 = (bf16[256,512]{1,0:T(8,128)(2,1)}, f32[8,512]{1,0:T(8,128)}) custom-call(bf16[256,512]{1,0:T(8,128)(2,1)S(1)} %get-tuple-element.4.grads, f32[8,512]{1,0:T(8,128)S(1)} %get-tuple-element.5.totals), custom_call_target="tpu_custom_call" | custom-call | tf_op jit(solution)/shard_map/put_out/pallas_call | solution.py:460
where the time goes:
time: 36.5 us; the launch traced here: 36.3 us
  Pallas kernels  35.7 us (98%)
  between operations  0.64 us (2%)
    pallas_call x1, Pallas kernels, fused_shards(): pl.pallas_call(attend_kernel, out_shape=(pltpu.VMEM((2 * HEAD_DIM, span_l...  35 us

commit v1 on v0

--- a/solution.py
+++ b/solution.py
@@ -162,11 +162,12 @@
 
 
 def attend_kernel(
-    lengths, queries, keys, values, out_grad,
+    lengths_hbm, queries, keys, values, out_grad,
     grads_out, totals_out,
-    query_buf, key_buf, value_buf, query_slots, key_ext, value_ext, grad_buf,
+    lengths, query_buf, key_buf, value_buf, query_slots, key_ext, value_ext, grad_buf,
     bias, key_acc, value_acc, halo_send, halo_recv, total_rows,
     local_sems, pair_send, pair_recv, query_send, query_recv, edge_send, edge_recv,
+    ready, span_ready,
 ):
     span = lax.axis_index("span")
     spans = lax.axis_size("span")
@@ -178,9 +179,9 @@
     piece_cols = 2 * HEAD_DIM
     pieces = head_cols // piece_cols
     width = WINDOW * BLOCK
-    swapped = me + 1 - 2 * lax.rem(me, 2)
-    order = (me, swapped, last - swapped, last - me)
-    targets = (last - swapped, swapped, last - me)
+    final = peers // 2 - me // (peers // 2)
+    second = 1 - jnp.minimum(me, 1)
+    order = (me, second, 6 - me - second - final, final)
 
     def column(index, size):
         return pl.ds(pl.multiple_of(index * size, size), size)
@@ -200,24 +201,37 @@
             queries.at[:, column(me, head_cols)], query_slots.at[me], local_sems.at[5]
         ),
         pltpu.make_async_copy(out_grad, grad_buf, local_sems.at[6]),
+        pltpu.make_async_copy(lengths_hbm, lengths, local_sems.at[7]),
     ]
     for load in loads:
         load.start()
 
     barrier = pltpu.get_barrier_semaphore()
-    for peer in order[1:]:
-        pl.semaphore_signal(barrier, inc=1, device_id={"head": peer}, device_id_type=MESH)
+    for peer in range(1, peers):
+
+        @pl.when(peer > me)
+        def _():
+            pl.semaphore_signal(barrier, inc=1, device_id={"head": peer}, device_id_type=MESH)
+
+    @pl.when(span < spans - 1)
+    def _():
+        pl.semaphore_signal(barrier, inc=1, device_id={"span": span + 1}, device_id_type=MESH)
+
+    @pl.when(me + span > 0)
+    def _():
+        pl.semaphore_wait(barrier, me + jnp.minimum(span, 1))
+
+    for peer in range(peers - 1):
+
+        @pl.when(peer < me)
+        def _():
+            pl.semaphore_signal(
+                ready.at[me], inc=1, device_id={"head": peer}, device_id_type=MESH
+            )
 
     @pl.when(span > 0)
     def _():
-        pl.semaphore_signal(barrier, inc=1, device_id={"span": span - 1}, device_id_type=MESH)
-
-    @pl.when(span < spans - 1)
-    def _():
-        pl.semaphore_signal(barrier, inc=1, device_id={"span": span + 1}, device_id_type=MESH)
-
-    neighbours = jnp.minimum(span, 1) + jnp.minimum(spans - 1 - span, 1)
-    pl.semaphore_wait(barrier, peers - 1 + neighbours)
+        pl.semaphore_signal(span_ready, inc=1, device_id={"span": span - 1}, device_id_type=MESH)
 
     def pair_copy(which, buf, ext, source, target):
         return pltpu.make_async_remote_copy(
@@ -239,24 +253,52 @@
             device_id_type=MESH,
         )
 
+    def send_pairs(peer):
+        pair_copy(0, key_buf, key_ext, me, peer).start()
+        pair_copy(1, value_buf, value_ext, me, peer).start()
+
+    def send_queries(peer):
+        for piece in range(pieces):
+            query_copy(piece, me, peer).start()
+
     loads[0].wait()
     loads[1].wait()
-    for peer in targets:
-        pair_copy(0, key_buf, key_ext, me, peer).start()
-        pair_copy(1, value_buf, value_ext, me, peer).start()
+    for peer in range(peers - 1):
+
+        @pl.when(peer < me)
+        def _():
+            send_pairs(peer)
+
     loads[2].wait()
-    for peer in targets:
-        for piece in range(pieces):
-            query_copy(piece, me, peer).start()
-
+    for peer in range(peers - 1):
+
+        @pl.when(peer < me)
+        def _():
+            send_queries(peer)
+
+    for peer in range(1, peers):
+
+        @pl.when(peer > me)
+        def _():
+            pl.semaphore_wait(ready.at[peer], 1)
+            send_pairs(peer)
+
+    for peer in reversed(range(1, peers)):
+
+        @pl.when(peer > me)
+        def _():
+            send_queries(peer)
 
     key_acc[...] = jnp.zeros_like(key_acc)
     value_acc[...] = jnp.zeros_like(value_acc)
     for load in loads[3:]:
         load.wait()
-    for peer in order[1:]:
-        pair_copy(0, key_buf, key_ext, peer, me).wait_recv()
-        pair_copy(1, value_buf, value_ext, peer, me).wait_recv()
+
+    def wait_pairs(peer):
+        @pl.when(peer != me)
+        def _():
+            pair_copy(0, key_buf, key_ext, peer, me).wait_recv()
+            pair_copy(1, value_buf, value_ext, peer, me).wait_recv()
 
     def halo_copy(which, ext):
         return pltpu.make_async_remote_copy(
@@ -277,10 +319,16 @@
         device_id_type=MESH,
     )
 
+    wait_pairs(last)
+
     @pl.when(span < spans - 1)
     def _():
+        pl.semaphore_wait(span_ready, 1)
         halo_copy(0, key_ext).start()
         halo_copy(1, value_ext).start()
+
+    for peer in range(last):
+        wait_pairs(peer)
 
     @pl.when(span > 0)
     def _():
@@ -304,6 +352,12 @@
         key_part = key_acc[held] * score_scale
         grads_out[pl.ds(0, HEAD_DIM), cols] = key_part.T.astype(jnp.bfloat16)
         grads_out[pl.ds(HEAD_DIM, HEAD_DIM), cols] = value_acc[held].T.astype(jnp.bfloat16)
+
+    def put_totals(block):
+        for head in range(2 * pieces):
+            totals_out[head : head + 1, block * BLOCK : (block + 1) * BLOCK] = total_rows[
+                block * pieces + head // 2, head % 2 : head % 2 + 1
+            ]
 
     for step in range(4):
         block = order[step]
@@ -357,6 +411,21 @@
                 def _():
                     write(done)
 
+            @pl.when(span < spans - 1)
+            def _():
+                return_copy.wait_recv()
+                held = pl.ds(last * BLOCK + HALO, BLOCK)
+                returned = halo_recv[...].astype(jnp.float32)
+                key_acc[held] += returned[:HALO]
+                value_acc[held] += returned[HALO:]
+
+            write(last)
+            for done in range(peers):
+
+                @pl.when(done != block)
+                def _():
+                    put_totals(done)
+
         lax.fori_loop(0, pieces, one_piece, 0)
 
         @pl.when((block == 0) & (span > 0))
@@ -365,27 +434,13 @@
             halo_send[pl.ds(HALO, HALO)] = value_acc[pl.ds(0, HALO)].astype(jnp.bfloat16)
             return_copy.start()
 
-    for block in range(peers):
-        for head in range(2 * pieces):
-            totals_out[head : head + 1, block * BLOCK : (block + 1) * BLOCK] = total_rows[
-                block * pieces + head // 2, head % 2 : head % 2 + 1
-            ]
-
-    for done in range(peers - 1):
-
-        @pl.when((done == order[3]) | (done == order[3] - 1))
-        def _():
+    for done in range(1, peers - 1):
+
+        @pl.when(done == final)
+        def _():
+            write(done - 1)
             write(done)
-
-    @pl.when(span < spans - 1)
-    def _():
-        return_copy.wait_recv()
-        held = pl.ds(last * BLOCK + HALO, BLOCK)
-        returned = halo_recv[...].astype(jnp.float32)
-        key_acc[held] += returned[:HALO]
-        value_acc[held] += returned[HALO:]
-
-    write(last)
+            put_totals(done)
 
     for peer in order[1:]:
         pair_copy(0, key_buf, key_ext, me, peer).wait_send()
@@ -430,9 +485,10 @@
             pltpu.VMEM((2 * HEAD_DIM, span_len), jnp.bfloat16),
             pltpu.VMEM((heads_here, span_len), jnp.float32),
         ),
-        in_specs=[pl.BlockSpec(memory_space=pltpu.SMEM)] + [any_space] * 4,
+        in_specs=[any_space] * 5,
         out_specs=(vmem, vmem),
         scratch_shapes=[
+            pltpu.SMEM(doc_lengths.shape, jnp.int32),
             pltpu.VMEM(queries.shape, jnp.bfloat16),
             pltpu.VMEM(keys.shape, jnp.bfloat16),
             pltpu.VMEM(values.shape, jnp.bfloat16),
@@ -446,13 +502,15 @@
             pltpu.VMEM((2 * HALO, HEAD_DIM), jnp.bfloat16),
             pltpu.VMEM((2 * HALO, HEAD_DIM), jnp.bfloat16),
             pltpu.VMEM((head_count * pieces, 8, BLOCK), jnp.float32),
-            dma((7,)),
+            dma((8,)),
             dma((2, head_count)),
             dma((2, head_count)),
             dma((head_count, pieces)),
             dma((head_count, pieces)),
             dma((3,)),
             dma((3,)),
+            pltpu.SemaphoreType.REGULAR((head_count,)),
+            pltpu.SemaphoreType.REGULAR,
         ],
         compiler_params=pltpu.CompilerParams(collective_id=0, has_side_effects=True),
         name="attend",

time: 36.5 us -> 34.3 us (0.940)
  the two profiles are of different devices: /device:TPU:25 before, /device:TPU:12 now
where the time goes in v1:
time: 34.3 us; the launch traced here: 34 us
  Pallas kernels  33.4 us (97%)
  between operations  0.64 us (2%)
    pallas_call x1, Pallas kernels, fused_shards(): pl.pallas_call(attend_kernel, out_shape=(pltpu.VMEM((2 * HEAD_DIM, span_l...  32.6 us
    pallas_call x1, Pallas kernels, fused_shards(): pl.pallas_call(put_out, out_shape=tuple((jax.ShapeDtypeStruct(one.shape,...  0.72 us

profile of v1, /device:TPU:12, one launch (start us, length us, event | category | flops | bytes accessed | tf_op | source)
XLA Modules:
  0.0 34.0 jit_solution(703899634316445741)
XLA Ops:
  0.6 32.6 %attend.1 = (bf16[256,512]{1,0:T(8,128)(2,1)S(1)}, f32[8,512]{1,0:T(8,128)S(1)}) custom-call(s32[4]{0:T(128)} %lengths_hbm.1, bf16[128,4096]{1,0:T(8,128)(2,1)} %queries.1, bf16[128,512]{1,0:T(8,128)(2,1)} %keys.1, bf16[128,512]{1,0:T(8,128)(2,1)} %values.1, bf16[512,1024]{1,0:T(8,128)(2,1)} %out_grad.1), custom_call_target="tpu_custom_call" | custom-call | tf_op jit(solution)/shard_map/attend/pallas_call | solution.py:482
  33.3 0.7 %put_out.1 = (bf16[256,512]{1,0:T(8,128)(2,1)}, f32[8,512]{1,0:T(8,128)}) custom-call(bf16[256,512]{1,0:T(8,128)(2,1)S(1)} %get-tuple-element.4.grads, f32[8,512]{1,0:T(8,128)S(1)} %get-tuple-element.5.totals), custom_call_target="tpu_custom_call" | custom-call | tf_op jit(solution)/shard_map/put_out/pallas_call | solution.py:518

commit v2 on v1

--- a/solution.py
+++ b/solution.py
@@ -179,9 +179,14 @@
     piece_cols = 2 * HEAD_DIM
     pieces = head_cols // piece_cols
     width = WINDOW * BLOCK
-    final = peers // 2 - me // (peers // 2)
-    second = 1 - jnp.minimum(me, 1)
-    order = (me, second, 6 - me - second - final, final)
+    def by_place(*choices):
+        pick = choices[0]
+        for place in range(1, len(choices)):
+            pick = jnp.where(me == place, choices[place], pick)
+        return pick
+
+    final = by_place(2, 2, 1, 1)
+    order = (by_place(0, 1, 2, 0), by_place(3, 0, 0, 3), by_place(1, 3, 3, 2), final)
 
     def column(index, size):
         return pl.ds(pl.multiple_of(index * size, size), size)
@@ -203,7 +208,7 @@
         pltpu.make_async_copy(out_grad, grad_buf, local_sems.at[6]),
         pltpu.make_async_copy(lengths_hbm, lengths, local_sems.at[7]),
     ]
-    for load in loads:
+    for load in loads[:3]:
         load.start()
 
     barrier = pltpu.get_barrier_semaphore()
@@ -257,8 +262,8 @@
         pair_copy(0, key_buf, key_ext, me, peer).start()
         pair_copy(1, value_buf, value_ext, me, peer).start()
 
-    def send_queries(peer):
-        for piece in range(pieces):
+    def send_queries(peer, some=range(pieces)):
+        for piece in some:
             query_copy(piece, me, peer).start()
 
     loads[0].wait()
@@ -283,19 +288,40 @@
             pl.semaphore_wait(ready.at[peer], 1)
             send_pairs(peer)
 
-    for peer in reversed(range(1, peers)):
+        if peer == peers // 2:
+
+            @pl.when(peer == me + 1)
+            def _():
+                send_queries(peer, range(1))
+
+    @pl.when(me == 0)
+    def _():
+        send_queries(1)
+
+    for peer in reversed(range(2, peers)):
 
         @pl.when(peer > me)
         def _():
-            send_queries(peer)
+            if peer == peers // 2:
+
+                @pl.when(peer > me + 1)
+                def _():
+                    send_queries(peer, range(1))
+
+                send_queries(peer, range(1, pieces))
+            else:
+                send_queries(peer)
+
+    for load in loads[3:]:
+        load.start()
 
     key_acc[...] = jnp.zeros_like(key_acc)
     value_acc[...] = jnp.zeros_like(value_acc)
     for load in loads[3:]:
         load.wait()
 
-    def wait_pairs(peer):
-        @pl.when(peer != me)
+    def wait_pairs(peer, wanted=True):
+        @pl.when((peer != me) & wanted)
         def _():
             pair_copy(0, key_buf, key_ext, peer, me).wait_recv()
             pair_copy(1, value_buf, value_ext, peer, me).wait_recv()
@@ -327,18 +353,6 @@
         halo_copy(0, key_ext).start()
         halo_copy(1, value_ext).start()
 
-    for peer in range(last):
-        wait_pairs(peer)
-
-    @pl.when(span > 0)
-    def _():
-        halo_copy(0, key_ext).wait_recv()
-        halo_copy(1, value_ext).wait_recv()
-
-    @pl.when(span == 0)
-    def _():
-        key_ext[pl.ds(0, HALO)] = jnp.zeros((HALO, HEAD_DIM), jnp.bfloat16)
-        value_ext[pl.ds(0, HALO)] = jnp.zeros((HALO, HEAD_DIM), jnp.bfloat16)
 
     score_scale = 1.0 / math.sqrt(HEAD_DIM)
     contract_last = (((1,), (1,)), ((), ()))
@@ -350,8 +364,8 @@
         held = pl.ds(HALO + done * BLOCK, BLOCK)
         cols = pl.ds(done * BLOCK, BLOCK)
         key_part = key_acc[held] * score_scale
-        grads_out[pl.ds(0, HEAD_DIM), cols] = key_part.T.astype(jnp.bfloat16)
-        grads_out[pl.ds(HEAD_DIM, HEAD_DIM), cols] = value_acc[held].T.astype(jnp.bfloat16)
+        grads_out[pl.ds(0, HEAD_DIM), cols] = key_part.astype(jnp.bfloat16).T
+        grads_out[pl.ds(HEAD_DIM, HEAD_DIM), cols] = value_acc[held].astype(jnp.bfloat16).T
 
     def put_totals(block):
         for head in range(2 * pieces):
@@ -361,6 +375,22 @@
 
     for step in range(4):
         block = order[step]
+        for peer in range(last):
+            known = False
+            for before in order[:step]:
+                known |= (before == peer) | (before == peer + 1)
+            wait_pairs(peer, ((block == peer) | (block == peer + 1)) & jnp.logical_not(known))
+
+        @pl.when((block == 0) & (span > 0))
+        def _():
+            halo_copy(0, key_ext).wait_recv()
+            halo_copy(1, value_ext).wait_recv()
+
+        @pl.when((block == 0) & (span == 0))
+        def _():
+            key_ext[pl.ds(0, HALO)] = jnp.zeros((HALO, HEAD_DIM), jnp.bfloat16)
+            value_ext[pl.ds(0, HALO)] = jnp.zeros((HALO, HEAD_DIM), jnp.bfloat16)
+
         first_row = pl.multiple_of(block * BLOCK, BLOCK)
         window = pl.ds(first_row, width)
         base = (span * peers + block) * BLOCK
@@ -375,8 +405,10 @@
         bias[...] = jnp.where(allowed, 0.0, -1e30)
 
         def one_piece(piece, carry, block=block, first_row=first_row, window=window, step=step):
-            if step > 0:
+            @pl.when(block != me)
+            def _():
                 query_copy(piece, block, me).wait_recv()
+
             cols = column(piece, piece_cols)
             query_pair = stacked(query_slots[block, :, cols])
             grad_pair = stacked(grad_buf[pl.ds(first_row, BLOCK), cols])
@@ -442,11 +474,14 @@
             write(done)
             put_totals(done)
 
-    for peer in order[1:]:
-        pair_copy(0, key_buf, key_ext, me, peer).wait_send()
-        pair_copy(1, value_buf, value_ext, me, peer).wait_send()
-        for piece in range(pieces):
-            query_copy(piece, me, peer).wait_send()
+    for peer in range(peers):
+
+        @pl.when(peer != me)
+        def _():
+            pair_copy(0, key_buf, key_ext, me, peer).wait_send()
+            pair_copy(1, value_buf, value_ext, me, peer).wait_send()
+            for piece in range(pieces):
+                query_copy(piece, me, peer).wait_send()
 
     @pl.when(span < spans - 1)
     def _():

time: 34.3 us -> 34.2 us (level)
  no operation moved by 1% of the time
where the time goes in v2:
time: 34.2 us; the launch traced here: 34 us
  Pallas kernels  33.3 us (97%)
  between operations  0.64 us (2%)
    pallas_call x1, Pallas kernels, fused_shards(): pl.pallas_call(attend_kernel, out_shape=(pltpu.VMEM((2 * HEAD_DIM, span_l...  32.6 us
    pallas_call x1, Pallas kernels, fused_shards(): pl.pallas_call(put_out, out_shape=tuple((jax.ShapeDtypeStruct(one.shape,...  0.72 us

profile of v2, /device:TPU:12, one launch (start us, length us, event | category | flops | bytes accessed | tf_op | source)
XLA Modules:
  0.0 34.0 jit_solution(8765717554661032023)
XLA Ops:
  0.6 32.6 %attend.1 = (bf16[256,512]{1,0:T(8,128)(2,1)S(1)}, f32[8,512]{1,0:T(8,128)S(1)}) custom-call(s32[4]{0:T(128)} %lengths_hbm.1, bf16[128,4096]{1,0:T(8,128)(2,1)} %queries.1, bf16[128,512]{1,0:T(8,128)(2,1)} %keys.1, bf16[128,512]{1,0:T(8,128)(2,1)} %values.1, bf16[512,1024]{1,0:T(8,128)(2,1)} %out_grad.1), custom_call_target="tpu_custom_call" | custom-call | tf_op jit(solution)/shard_map/attend/pallas_call | solution.py:517
  33.3 0.7 %put_out.1 = (bf16[256,512]{1,0:T(8,128)(2,1)}, f32[8,512]{1,0:T(8,128)}) custom-call(bf16[256,512]{1,0:T(8,128)(2,1)S(1)} %get-tuple-element.4.grads, f32[8,512]{1,0:T(8,128)S(1)} %get-tuple-element.5.totals), custom_call_target="tpu_custom_call" | custom-call | tf_op jit(solution)/shard_map/put_out/pallas_call | solution.py:553

commit v3 on v2

--- a/solution.py
+++ b/solution.py
@@ -166,7 +166,7 @@
     grads_out, totals_out,
     lengths, query_buf, key_buf, value_buf, query_slots, key_ext, value_ext, grad_buf,
     bias, key_acc, value_acc, halo_send, halo_recv, total_rows,
-    local_sems, pair_send, pair_recv, query_send, query_recv, edge_send, edge_recv,
+    local_sems, pair_send, pair_recv, query_send, query_recv, whole_send, whole_recv, edge_send, edge_recv,
     ready, span_ready,
 ):
     span = lax.axis_index("span")
@@ -186,7 +186,7 @@
         return pick
 
     final = by_place(2, 2, 1, 1)
-    order = (by_place(0, 1, 2, 0), by_place(3, 0, 0, 3), by_place(1, 3, 3, 2), final)
+    order = (by_place(0, 1, 2, 3), by_place(3, 0, 0, 2), by_place(1, 3, 3, 0), final)
 
     def column(index, size):
         return pl.ds(pl.multiple_of(index * size, size), size)
@@ -252,8 +252,8 @@
         return pltpu.make_async_remote_copy(
             src_ref=query_buf.at[:, column(target * pieces + piece, piece_cols)],
             dst_ref=query_slots.at[source, :, column(piece, piece_cols)],
-            send_sem=query_send.at[target, piece],
-            recv_sem=query_recv.at[source, piece],
+            send_sem=query_send.at[piece],
+            recv_sem=query_recv.at[piece],
             device_id={"head": target},
             device_id_type=MESH,
         )
@@ -262,55 +262,65 @@
         pair_copy(0, key_buf, key_ext, me, peer).start()
         pair_copy(1, value_buf, value_ext, me, peer).start()
 
-    def send_queries(peer, some=range(pieces)):
+    def whole_copy(source, target):
+        return pltpu.make_async_remote_copy(
+            src_ref=query_buf.at[:, column(target, head_cols)],
+            dst_ref=query_slots.at[source],
+            send_sem=whole_send.at[target],
+            recv_sem=whole_recv.at[source],
+            device_id={"head": target},
+            device_id_type=MESH,
+        )
+
+    middle = (me > 0) & (me < last)
+
+    def send_pieces(some):
         for piece in some:
-            query_copy(piece, me, peer).start()
+            query_copy(piece, me, last - me).start()
+
+    def send_up_pairs(peer):
+        @pl.when(peer > me)
+        def _():
+            pl.semaphore_wait(ready.at[peer], 1)
+            send_pairs(peer)
+
+    def send_whole(peer, wanted):
+        @pl.when(wanted)
+        def _():
+            whole_copy(me, peer).start()
 
     loads[0].wait()
     loads[1].wait()
-    for peer in range(peers - 1):
+    for peer in range(last):
 
         @pl.when(peer < me)
         def _():
             send_pairs(peer)
 
     loads[2].wait()
-    for peer in range(peers - 1):
-
-        @pl.when(peer < me)
-        def _():
-            send_queries(peer)
-
-    for peer in range(1, peers):
-
-        @pl.when(peer > me)
-        def _():
-            pl.semaphore_wait(ready.at[peer], 1)
-            send_pairs(peer)
-
-        if peer == peers // 2:
-
-            @pl.when(peer == me + 1)
-            def _():
-                send_queries(peer, range(1))
-
-    @pl.when(me == 0)
-    def _():
-        send_queries(1)
-
-    for peer in reversed(range(2, peers)):
-
-        @pl.when(peer > me)
-        def _():
-            if peer == peers // 2:
-
-                @pl.when(peer > me + 1)
-                def _():
-                    send_queries(peer, range(1))
-
-                send_queries(peer, range(1, pieces))
-            else:
-                send_queries(peer)
+    send_whole(0, me > 1)
+    send_whole(1, me == last)
+    send_whole(2, me == last)
+    send_up_pairs(1)
+    send_up_pairs(2)
+
+    @pl.when(me == 1)
+    def _():
+        send_pieces(range(1))
+
+    send_up_pairs(last)
+    send_whole(1, me == 0)
+    send_whole(2, me == 0)
+    send_whole(last, me < last)
+    send_whole(0, me == 1)
+
+    @pl.when(me == 1)
+    def _():
+        send_pieces(range(1, pieces))
+
+    @pl.when(me == 2)
+    def _():
+        send_pieces(range(pieces))
 
     for load in loads[3:]:
         load.start()
@@ -372,6 +382,17 @@
             totals_out[head : head + 1, block * BLOCK : (block + 1) * BLOCK] = total_rows[
                 block * pieces + head // 2, head % 2 : head % 2 + 1
             ]
+
+    def take_return():
+        @pl.when(span < spans - 1)
+        def _():
+            return_copy.wait_recv()
+            held = pl.ds(last * BLOCK + HALO, BLOCK)
+            returned = halo_recv[...].astype(jnp.float32)
+            key_acc[held] += returned[:HALO]
+            value_acc[held] += returned[HALO:]
+
+        write(last)
 
     for step in range(4):
         block = order[step]
@@ -405,9 +426,11 @@
         bias[...] = jnp.where(allowed, 0.0, -1e30)
 
         def one_piece(piece, carry, block=block, first_row=first_row, window=window, step=step):
-            @pl.when(block != me)
-            def _():
-                query_copy(piece, block, me).wait_recv()
+            if step == 3:
+
+                @pl.when(middle)
+                def _():
+                    query_copy(piece, block, me).wait_recv()
 
             cols = column(piece, piece_cols)
             query_pair = stacked(query_slots[block, :, cols])
@@ -423,9 +446,11 @@
             row_max = jnp.max(scores, axis=0, keepdims=True)
             exponent = jnp.exp2(scores - row_max)
             row_total = jnp.sum(exponent, axis=0, keepdims=True)
-            weights = exponent * (1.0 / row_total)
+            mixed = jnp.sum(exponent * dweights, axis=0, keepdims=True)
+            inverse = 1.0 / row_total
+            weights = exponent * inverse
             weights_low = weights.astype(jnp.bfloat16)
-            delta = jnp.sum(weights * dweights, axis=0, keepdims=True)
+            delta = mixed * inverse
             dscores = (weights * (dweights - delta)).astype(jnp.bfloat16)
             key_acc[window] += jnp.dot(dscores, query_pair, preferred_element_type=jnp.float32)
             value_acc[window] += jnp.dot(weights_low, grad_pair, preferred_element_type=jnp.float32)
@@ -443,21 +468,17 @@
                 def _():
                     write(done)
 
-            @pl.when(span < spans - 1)
-            def _():
-                return_copy.wait_recv()
-                held = pl.ds(last * BLOCK + HALO, BLOCK)
-                returned = halo_recv[...].astype(jnp.float32)
-                key_acc[held] += returned[:HALO]
-                value_acc[held] += returned[HALO:]
-
-            write(last)
+            pl.when(me < last)(take_return)
             for done in range(peers):
 
                 @pl.when(done != block)
                 def _():
                     put_totals(done)
 
+        @pl.when((block != me) & jnp.logical_not(middle & (step == 3)))
+        def _():
+            whole_copy(block, me).wait_recv()
+
         lax.fori_loop(0, pieces, one_piece, 0)
 
         @pl.when((block == 0) & (span > 0))
@@ -466,6 +487,7 @@
             halo_send[pl.ds(HALO, HALO)] = value_acc[pl.ds(0, HALO)].astype(jnp.bfloat16)
             return_copy.start()
 
+    pl.when(me == last)(take_return)
     for done in range(1, peers - 1):
 
         @pl.when(done == final)
@@ -480,8 +502,15 @@
         def _():
             pair_copy(0, key_buf, key_ext, me, peer).wait_send()
             pair_copy(1, value_buf, value_ext, me, peer).wait_send()
-            for piece in range(pieces):
-                query_copy(piece, me, peer).wait_send()
+
+            @pl.when(jnp.logical_not(middle & (peer == last - me)))
+            def _():
+                whole_copy(me, peer).wait_send()
+
+    @pl.when(middle)
+    def _():
+        for piece in range(pieces):
+            query_copy(piece, me, last - me).wait_send()
 
     @pl.when(span < spans - 1)
     def _():
@@ -540,8 +569,10 @@
             dma((8,)),
             dma((2, head_count)),
             dma((2, head_count)),
-            dma((head_count, pieces)),
-            dma((head_count, pieces)),
+            dma((pieces,)),
+            dma((pieces,)),
+            dma((head_count,)),
+            dma((head_count,)),
             dma((3,)),
             dma((3,)),
             pltpu.SemaphoreType.REGULAR((head_count,)),

time: 34.2 us -> 34 us (level)
  no operation moved by 1% of the time
where the time goes in v3:
time: 34 us; the launch traced here: 33.8 us
  Pallas kernels  33.2 us (98%)
  between operations  0.64 us (2%)
    pallas_call x1, Pallas kernels, fused_shards(): pl.pallas_call(attend_kernel, out_shape=(pltpu.VMEM((2 * HEAD_DIM, span_l...  32.4 us
    pallas_call x1, Pallas kernels, fused_shards(): pl.pallas_call(put_out, out_shape=tuple((jax.ShapeDtypeStruct(one.shape,...  0.72 us

profile of v3, /device:TPU:12, one launch (start us, length us, event | category | flops | bytes accessed | tf_op | source)
XLA Modules:
  0.0 33.8 jit_solution(13825637719367493370)
XLA Ops:
  0.6 32.4 %attend.1 = (bf16[256,512]{1,0:T(8,128)(2,1)S(1)}, f32[8,512]{1,0:T(8,128)S(1)}) custom-call(s32[4]{0:T(128)} %lengths_hbm.1, bf16[128,4096]{1,0:T(8,128)(2,1)} %queries.1, bf16[128,512]{1,0:T(8,128)(2,1)} %keys.1, bf16[128,512]{1,0:T(8,128)(2,1)} %values.1, bf16[512,1024]{1,0:T(8,128)(2,1)} %out_grad.1), custom_call_target="tpu_custom_call" | custom-call | tf_op jit(solution)/shard_map/attend/pallas_call | solution.py:546
  33.1 0.7 %put_out.1 = (bf16[256,512]{1,0:T(8,128)(2,1)}, f32[8,512]{1,0:T(8,128)}) custom-call(bf16[256,512]{1,0:T(8,128)(2,1)S(1)} %get-tuple-element.4.grads, f32[8,512]{1,0:T(8,128)S(1)} %get-tuple-element.5.totals), custom_call_target="tpu_custom_call" | custom-call | tf_op jit(solution)/shard_map/put_out/pallas_call | solution.py:584
